TPU v7x, 32 devices: a whole 2x2x4 slice. The times are simulated.
32 devices in a mesh: orb: 16 (over z, y, core), grid: 2 (over x).
Axes of the slice: x: 2, y: 2, z: 4, core: 2. Of those that a mesh axis runs over, the one named last changes fastest.
Arguments:
- orbitals: bfloat16 [32, 11520], P('orb', 'grid'), may hold values from -1.5 to 1.5
- occupation: bfloat16 [32], P('orb'), may hold values from 0.29882812 to 1
Outputs:
- potentials: float32 [32, 11520], P('orb', 'grid')
- projectors: float32 [32, 11520], P('orb', 'grid')
All inputs are finite; a program needn't handle non-finite values.
Results may differ from a plain program's by a relative error of at most 0.0025.
Values may be sent and summed in bfloat16 or wider, within the bound.
No kernel may reach another device: no remote copies, remote signals or barrier semaphores. Data moves between devices by JAX's collectives and lax.ppermute only.
A program may use at most 64 MiB of HBM per device.

v0:
```python
import math
import jax
import jax.numpy as jnp
from jax import lax
from jax.sharding import PartitionSpec as P

NX = 20
NY = 24
NZ = 24
NPTS = 11520


def hartley_table(length):
    index = jnp.arange(length, dtype=jnp.int32)
    product = index[:, None] * index[None, :] % length
    angle = 2.0 * math.pi / length * product.astype(jnp.float32)
    return (jnp.cos(angle) + jnp.sin(angle)).astype(jnp.bfloat16)


def signed_square(length):
    index = jnp.arange(length, dtype=jnp.int32)
    signed = jnp.where(index <= length // 2, index, index - length).astype(jnp.float32)
    return (2.0 * math.pi * signed / length) ** 2


def coulomb_kernel(size_x, size_y, size_z):
    total = (
        signed_square(size_x)[:, None, None]
        + signed_square(size_y)[None, :, None]
        + signed_square(size_z)[None, None, :]
    )
    safe = jnp.where(total > 0, total, 1.0)
    return jnp.where(total > 0, 1.0 / safe, 0.0) / (size_x * size_y * size_z)


def solve_pairs(density, table_x, table_y, table_z, kernel):
    section = jnp.einsum(
        "ax,pxyz->payz", table_x, density, preferred_element_type=jnp.float32
    ).astype(jnp.bfloat16)
    section = jnp.einsum(
        "by,pxyz->pxbz", table_y, section, preferred_element_type=jnp.float32
    ).astype(jnp.bfloat16)
    spectrum = jnp.einsum("cz,pxyz->pxyc", table_z, section, preferred_element_type=jnp.float32)
    section = (spectrum * kernel).astype(jnp.bfloat16)
    section = jnp.einsum(
        "cz,pxyz->pxyc", table_z, section, preferred_element_type=jnp.float32
    ).astype(jnp.bfloat16)
    section = jnp.einsum(
        "by,pxyz->pxbz", table_y, section, preferred_element_type=jnp.float32
    ).astype(jnp.bfloat16)
    return jnp.einsum("ax,pxyz->payz", table_x, section, preferred_element_type=jnp.float32)


def pair_folder(targets, running, pieces):
    table_x = hartley_table(NX)
    table_y = hartley_table(NY)
    table_z = hartley_table(NZ)
    kernel = coulomb_kernel(NX, NY, NZ)
    target_rows = targets.astype(jnp.float32)
    target_count = targets.shape[0]
    block, block_weight = pieces
    rows = block.shape[0]
    group = math.gcd(rows, 64)
    blocks = block.reshape(rows // group, group, NPTS)
    weights = block_weight.astype(jnp.float32).reshape(rows // group, group)

    def accumulate(totals, inputs):
        sources, source_weight = inputs
        source_rows = sources.astype(jnp.float32)
        density = (target_rows[:, None, :] * source_rows[None, :, :]).astype(jnp.bfloat16)
        density = density.reshape(target_count * group, NX, NY, NZ)
        potential = solve_pairs(density, table_x, table_y, table_z, kernel).reshape(
            target_count, group, NPTS
        )
        weighted = source_weight[None, :, None] * potential * source_rows[None, :, :]
        return (totals - jnp.sum(weighted, axis=1), None)

    result, unused = lax.scan(accumulate, running, (blocks, weights))
    return result


def on_device(orbitals, occupation):
    own_count = orbitals.shape[0]
    per_device = own_count // lax.axis_size("grid")
    empty = jnp.zeros((per_device, NPTS), jnp.float32)
    whole = lax.all_gather(orbitals, "grid", axis=1, tiled=True)
    targets = lax.dynamic_slice_in_dim(whole, lax.axis_index("grid") * per_device, per_device, 0)
    totals = pair_folder(
        targets,
        empty,
        (
            lax.all_gather(whole, "orb", axis=0, tiled=True),
            lax.all_gather(occupation, "orb", axis=0, tiled=True),
        ),
    )
    potentials = lax.all_to_all(totals, "grid", split_axis=1, concat_axis=0, tiled=True)
    source_points, potential_points = (
        lax.all_to_all(
            orbitals.astype(jnp.float32), "orb", split_axis=1, concat_axis=0, tiled=True
        ),
        lax.all_to_all(potentials, "orb", split_axis=1, concat_axis=0, tiled=True),
    )
    partial_gram = (
        lax.dot_general(
            source_points,
            potential_points,
            (((1,), (1,)), ((), ())),
            precision=lax.Precision.HIGHEST,
        )
        / NPTS
    )
    gram = lax.psum(partial_gram, ("orb", "grid"))
    factor = jnp.linalg.cholesky(-gram)
    identity = jnp.eye(gram.shape[0], dtype=jnp.float32)
    inverse = lax.linalg.triangular_solve(factor, identity, left_side=True, lower=True)
    projector_points = jnp.dot(inverse, potential_points, precision=lax.Precision.HIGHEST)
    projectors = lax.all_to_all(projector_points, "orb", split_axis=0, concat_axis=1, tiled=True)
    return (potentials, projectors)


def solution(mesh):
    placed = (P("orb", "grid"), P("orb"))
    return jax.shard_map(
        on_device,
        mesh=mesh,
        in_specs=placed,
        out_specs=(P("orb", "grid"), P("orb", "grid")),
        check_vma=False,
    )
```

profile of v0, /device:TPU:0, one launch (start us, length us, event | category | flops | bytes accessed | tf_op | source)
XLA Modules:
  0.0 226.1 jit_solution(919936937522886090)
XLA Ops:
  0.7 5.7 %all_gather.10 = bf16[2,11520]{1,0:T(2,128)(2,1)S(1)} all-gather(bf16[2,5760]{1,0:T(2,128)(2,1)} %param.2), channel_id=1, replica_groups=mesh['orb'=16,'grid'=2] {'grid'}, dimensions={1}, use_global_device_ids=true | all-gather | bytes 69120 | tf_op jit(solution)/shard_map/all_gather | solution.py:86
  6.3 24.3 %all-gather = bf16[16,2,11520]{2,1,0:T(2,128)(2,1)S(1)} all-gather(bf16[1,2,11520]{2,1,0:T(2,128)(2,1)S(1)} %bitcast.58), channel_id=1, replica_groups=mesh['orb'=16,'grid'=2] {'orb'}, dimensions={0}, use_global_device_ids=true | all-gather | bytes 783360 | tf_op jit(solution)/shard_map/all_gather | solution.py:92
  30.7 6.4 %reshape.167 = f32[32,20,24,24]{3,2,1,0:T(8,128)} reshape(bf16[16,2,11520]{2,1,0:T(2,128)(2,1)S(1)} %all-gather) | data formatting | bytes 2211840 | tf_op jit(solution)/shard_map/while/body/eval_jaxpr/convert_element_type | solution.py:69
  37.1 1.3 reshape.174
  38.4 0.1 convert_reduce_fusion
  38.6 0.2 reshape.166
  38.8 3.9 %multiply_convert_fusion.1 = bf16[32,20,24,24]{3,2,1,0:T(8,128)(2,1)S(1)} fusion(f32[32,20,24,24]{3,2,1,0:T(8,128)} %reshape.167, f32[20,24,24]{2,1,0:T(8,128)S(1)} %reshape.166), kind=kLoop, calls=%fused_computation.1 | loop fusion | flops 737280 | bytes 2257920 | tf_op jit(solution)/shard_map/while/body/eval_jaxpr/convert_element_type | solution.py:70
  42.6 4.9 %convert_bitcast_fusion = bf16[32,20,24,24]{1,3,2,0:T(8,128)(2,1)} fusion(bf16[32,20,24,24]{3,2,1,0:T(8,128)(2,1)S(1)} %multiply_convert_fusion.1), kind=kOutput, calls=%fused_computation.4 | convolution fusion | flops 15118640 | bytes 1474560 | tf_op jit(solution)/shard_map/while/body/eval_jaxpr/ax,pxyz->payz/dot_general | solution.py:37
  47.5 8.5 %copy.24 = bf16[32,20,24,24]{2,3,1,0:T(8,128)(2,1)} copy(bf16[32,20,24,24]{1,3,2,0:T(8,128)(2,1)} %convert_bitcast_fusion) | data formatting | bytes 1474560 | tf_op jit(solution)/shard_map/while/body/eval_jaxpr/convert_element_type | solution.py:39
  56.0 5.2 %fusion.44 = bf16[32,20,24,24]{3,2,1,0:T(8,128)(2,1)} fusion(bf16[32,20,24,24]{2,3,1,0:T(8,128)(2,1)} %copy.24), kind=kOutput, calls=%fused_computation.53 | convolution fusion | flops 17701056 | bytes 1474560 | tf_op jit(solution)/shard_map/while/body/eval_jaxpr/by,pxyz->pxbz/dot_general | solution.py:40
  61.3 0.1 fusion.19
  61.5 7.4 %fusion.2 = bf16[32,20,24,24]{3,2,1,0:T(8,128)(2,1)} fusion(f32[20,24,24]{2,1,0:T(8,128)S(1)} %fusion.19, bf16[32,20,24,24]{3,2,1,0:T(8,128)(2,1)} %fusion.44), kind=kOutput, calls=%fused_computation.5 | convolution fusion | flops 36139392 | bytes 1520640 | tf_op jit(solution)/shard_map/while/body/eval_jaxpr/cz,pxyz->pxyc/dot_general | solution.py:45
  68.9 5.4 %convert_bitcast_fusion.1 = bf16[32,20,24,24]{2,3,1,0:T(8,128)(2,1)} fusion(bf16[32,20,24,24]{3,2,1,0:T(8,128)(2,1)} %fusion.2), kind=kOutput, calls=%fused_computation.8 | convolution fusion | flops 18069696 | bytes 1474560 | tf_op jit(solution)/shard_map/while/body/eval_jaxpr/by,pxyz->pxbz/dot_general | solution.py:48
  74.3 10.1 %copy.27 = bf16[32,20,24,24]{0,1,3,2:T(8,128)(2,1)S(1)} copy(bf16[32,20,24,24]{2,3,1,0:T(8,128)(2,1)} %convert_bitcast_fusion.1) | data formatting | bytes 1474560 | tf_op jit(solution)/shard_map/while/body/eval_jaxpr/convert_element_type | solution.py:50
  84.4 4.0 %convolution_bitcast_fusion = f32[32,20,24,24]{0,1,3,2:T(8,128)} fusion(bf16[32,20,24,24]{0,1,3,2:T(8,128)(2,1)S(1)} %copy.27), kind=kOutput, calls=%fused_computation.13 | convolution fusion | flops 14750000 | bytes 2211840 | tf_op jit(solution)/shard_map/while/body/eval_jaxpr/ax,pxyz->payz/dot_general | solution.py:51
  88.4 12.1 %copy.28 = f32[32,20,24,24]{3,2,1,0:T(8,128)} copy(f32[32,20,24,24]{0,1,3,2:T(8,128)} %convolution_bitcast_fusion) | data formatting | bytes 2949120 | tf_op jit(solution)/shard_map/while/body/eval_jaxpr/ax,pxyz->payz/transpose | solution.py:51
  100.5 0.6 dynamic-slice
  101.8 0.2 dynamic-update-slice.3
  102.0 6.8 %reshape.165 = f32[32,11520]{1,0:T(8,128)S(1)} reshape(f32[32,20,24,24]{3,2,1,0:T(8,128)} %copy.28) | data formatting | bytes 2949120 | tf_op jit(solution)/shard_map/while/body/eval_jaxpr/reshape | solution.py:72
  108.9 29.9 %all-reduce = bf16[32]{0:T(256)(128)(2,1)S(1)} all-reduce(bf16[32]{0:T(256)(128)(2,1)S(1)} %dynamic-update-slice.3), channel_id=1, replica_groups=mesh['orb'=16,'grid'=2] {'orb'}, use_global_device_ids=true, to_apply=%add | all-reduce | flops 32 | bytes 128
  138.8 0.3 multiply_reduce_fusion
  139.1 0.7 sub.25
  139.7 3.3 %all-to-all-start = ((f32[1,2,5760]{2,0,1:T(1,128)}), f32[1,2,5760]{2,0,1:T(1,128)S(1)}, u32[]{:S(2)}, u32[]{:S(2)}) async-start(f32[1,2,5760]{2,0,1:T(1,128)} %sub.25), calls=%async_computation | async-start | bytes 92160 | tf_op jit(solution)/shard_map/all_to_all | solution.py:96
  143.0 0.1 reshape.168
  143.2 0.6 copy.30
  143.8 3.2 %all-to-all-done = f32[1,2,5760]{2,0,1:T(1,128)S(1)} async-done(((f32[1,2,5760]{2,0,1:T(1,128)}), f32[1,2,5760]{2,0,1:T(1,128)S(1)}, u32[]{:S(2)}, u32[]{:S(2)}) %all-to-all-start) | async-done | bytes 46112 | tf_op jit(solution)/shard_map/all_to_all | solution.py:96
  147.0 3.5 %all-to-all-start.2 = ((f32[2,16,360]{2,0,1:T(2,128)}), f32[2,16,360]{2,0,1:T(2,128)S(1)}, u32[]{:S(2)}, u32[]{:S(2)}) async-start(f32[2,16,360]{2,0,1:T(2,128)} %copy.30), calls=%async_computation.2 | async-start | bytes 98304 | tf_op jit(solution)/shard_map/all_to_all | solution.py:98
  150.5 0.1 reduce.11
  150.7 0.1 all_to_all.54
  150.8 0.6 copy.29
  151.4 5.8 %all-to-all-done.2 = f32[2,16,360]{2,0,1:T(2,128)S(1)} async-done(((f32[2,16,360]{2,0,1:T(2,128)}), f32[2,16,360]{2,0,1:T(2,128)S(1)}, u32[]{:S(2)}, u32[]{:S(2)}) %all-to-all-start.2) | async-done | bytes 46112 | tf_op jit(solution)/shard_map/all_to_all | solution.py:98
  157.3 3.5 %all-to-all-start.1 = ((f32[2,16,360]{2,0,1:T(2,128)}), f32[2,16,360]{2,0,1:T(2,128)S(1)}, u32[]{:S(2)}, u32[]{:S(2)}) async-start(f32[2,16,360]{2,0,1:T(2,128)} %copy.29), calls=%async_computation.1 | async-start | bytes 98304 | tf_op jit(solution)/shard_map/all_to_all | solution.py:101
  160.8 6.7 %all-to-all-done.1 = f32[2,16,360]{2,0,1:T(2,128)S(1)} async-done(((f32[2,16,360]{2,0,1:T(2,128)}), f32[2,16,360]{2,0,1:T(2,128)S(1)}, u32[]{:S(2)}, u32[]{:S(2)}) %all-to-all-start.1) | async-done | bytes 46112 | tf_op jit(solution)/shard_map/all_to_all | solution.py:101
  167.6 0.2 fusion.17
  167.8 38.0 %psum.7 = f32[32,32]{0,1:T(8,128)S(1)} all-reduce(f32[32,32]{0,1:T(8,128)S(1)} %fusion.17), channel_id=1, replica_groups=mesh['orb'=16,'grid'=2] {'orb','grid'}, use_global_device_ids=true, to_apply=%region_1.2 | all-reduce | flops 1024 | bytes 8192 | tf_op jit(solution)/shard_map/psum | solution.py:112
  205.8 0.1 copy.31
  205.8 2.9 %cholesky.17 = f32[32,32]{1,0:T(8,128)S(1)} custom-call(f32[32,32]{1,0:T(8,128)S(1)} %fusion.22), custom_call_target="Cholesky" | custom-call | tf_op jit(solution)/shard_map/jit(cholesky)/cholesky | solution.py:113
  208.8 0.6 compare_reduce_fusion
  209.4 0.7 fusion.21
  210.1 2.4 %custom-call.6 = f32[1,32,32]{1,2,0:T(8,128)S(1)} custom-call(f32[1,32,32]{2,1,0:T(8,128)S(1)} %fusion.21), custom_call_target="InvertDiagBlocksLowerTriangular" | custom-call | tf_op jit(solution)/shard_map/triangular_solve | solution.py:115
  212.5 0.1 copy.32
  212.6 0.2 fusion.23
  212.8 0.2 fusion.88
  213.0 0.6 copy.34
  213.6 5.0 %all-to-all-start.3 = ((f32[16,2,360]{2,1,0:T(2,128)}), f32[16,2,360]{2,1,0:T(2,128)S(1)}, u32[]{:S(2)}, u32[]{:S(2)}) async-start(f32[16,2,360]{2,1,0:T(2,128)} %copy.34), calls=%async_computation.3 | async-start | bytes 98304 | tf_op jit(solution)/shard_map/all_to_all | solution.py:117
  218.6 0.6 copy.48
  219.3 6.1 %all-to-all-done.3 = f32[16,2,360]{2,1,0:T(2,128)S(1)} async-done(((f32[16,2,360]{2,1,0:T(2,128)}), f32[16,2,360]{2,1,0:T(2,128)S(1)}, u32[]{:S(2)}, u32[]{:S(2)}) %all-to-all-start.3) | async-done | bytes 46112 | tf_op jit(solution)/shard_map/all_to_all | solution.py:117
  225.4 0.8 all_to_all.65
  (21 shorter events, 0.3 us)
Async XLA Ops:
  88.4 12.1 %copy-start.3 = (u32[32]{0:T(128)S(1)}, u32[32]{0:T(128)}, u32[]{:S(2)}) copy-start(u32[32]{0:T(128)} %constant.125) | copy-start | bytes 388
  88.4 13.4 %copy-start.2 = (bf16[2]{0:T(256)(128)(2,1)S(1)}, bf16[2]{0:T(256)(128)(2,1)}, u32[]{:S(2)}) copy-start(bf16[2]{0:T(256)(128)(2,1)} %param.3) | copy-start | bytes 16
  102.0 36.7 %copy-start = (f32[32,11520]{1,0:T(8,128)S(1)}, f32[32,11520]{1,0:T(8,128)}, u32[]{:S(2)}) copy-start(f32[32,11520]{1,0:T(8,128)} %reshape.174) | copy-start | bytes 4423684
  102.0 41.0 %copy-start.1 = (bf16[2,5760]{1,0:T(2,128)(2,1)S(1)}, bf16[2,5760]{1,0:T(2,128)(2,1)}, u32[]{:S(2)}) copy-start(bf16[2,5760]{1,0:T(2,128)(2,1)} %param.2) | copy-start | bytes 69124
  139.7 7.3 %all-to-all-start = ((f32[1,2,5760]{2,0,1:T(1,128)}), f32[1,2,5760]{2,0,1:T(1,128)S(1)}, u32[]{:S(2)}, u32[]{:S(2)}) async-start(f32[1,2,5760]{2,0,1:T(1,128)} %sub.25), calls=%async_computation | async-start | bytes 92160 | tf_op jit(solution)/shard_map/all_to_all | solution.py:96
  147.0 10.2 %all-to-all-start.2 = ((f32[2,16,360]{2,0,1:T(2,128)}), f32[2,16,360]{2,0,1:T(2,128)S(1)}, u32[]{:S(2)}, u32[]{:S(2)}) async-start(f32[2,16,360]{2,0,1:T(2,128)} %copy.30), calls=%async_computation.2 | async-start | bytes 98304 | tf_op jit(solution)/shard_map/all_to_all | solution.py:98
  157.3 10.2 %all-to-all-start.1 = ((f32[2,16,360]{2,0,1:T(2,128)}), f32[2,16,360]{2,0,1:T(2,128)S(1)}, u32[]{:S(2)}, u32[]{:S(2)}) async-start(f32[2,16,360]{2,0,1:T(2,128)} %copy.29), calls=%async_computation.1 | async-start | bytes 98304 | tf_op jit(solution)/shard_map/all_to_all | solution.py:101
  213.6 11.8 %all-to-all-start.3 = ((f32[16,2,360]{2,1,0:T(2,128)}), f32[16,2,360]{2,1,0:T(2,128)S(1)}, u32[]{:S(2)}, u32[]{:S(2)}) async-start(f32[16,2,360]{2,1,0:T(2,128)} %copy.34), calls=%async_computation.3 | async-start | bytes 98304 | tf_op jit(solution)/shard_map/all_to_all | solution.py:117
where the time goes:
time: 227 us; the launch traced here: 226 us
  blocking collectives  97.9 us (43%)
  local copies, waits for them, and re-layouts  50.8 us (22%)
  matrix products  27.5 us (12%)
  waiting for transfers between devices  21.9 us (10%)
  starting transfers between devices  15.3 us (7%)
  other arithmetic  11.4 us (5%)
    psum x1, blocking collectives, on_device(): gram = lax.psum(partial_gram, ('orb', 'grid'))  38 us
    unnamed x1, blocking collectives  29.9 us
    all_gather x1, blocking collectives, on_device(): lax.all_gather(whole, 'orb', axis=0, tiled=True)  24.3 us
    transpose x1, local copies, waits for them, and re-layouts, solve_pairs(): jnp.einsum('ax,pxyz->payz', table_x, section, preferred_element_type=jnp....  12.1 us
    dot_general x2, matrix products, solve_pairs(): jnp.einsum('by,pxyz->pxbz', table_y, section, preferred_element_type=jnp....  10.6 us
    convert_element_type x1, local copies, waits for them, and re-layouts, solve_pairs(): section = jnp.einsum('by,pxyz->pxbz', table_y, section, preferred_element...  10.1 us
    convert_element_type x1, local copies, waits for them, and re-layouts, solve_pairs(): section = jnp.einsum('ax,pxyz->payz', table_x, density, preferred_element...  8.51 us
    convert_element_type x2, local copies, waits for them, and re-layouts, accumulate(): source_rows = sources.astype(jnp.float32)  7.76 us
  transfers between devices with their start and end apart: 4, of which 4 were waited for; matrix products, arithmetic and copies ran while one was open for 1% of the time, Pallas kernels for 0%

commit v1 on v0

--- a/solution.py
+++ b/solution.py
@@ -109,7 +109,7 @@
         )
         / NPTS
     )
-    gram = lax.psum(partial_gram, ("orb", "grid"))
+    gram = lax.psum(lax.psum(partial_gram, "grid"), "orb")
     factor = jnp.linalg.cholesky(-gram)
     identity = jnp.eye(gram.shape[0], dtype=jnp.float32)
     inverse = lax.linalg.triangular_solve(factor, identity, left_side=True, lower=True)

time: 227 us -> 252 us (1.11)
  blocking collectives: 97.9 us -> 124 us
    psum x1 -> x2, blocking collectives: 38 us -> 64.3 us  [on_device(): gram = lax.psum(lax.psum(partial_gram, 'grid'), 'orb')]
where the time goes in v1:
time: 252 us; the launch traced here: 251 us
  blocking collectives  124 us (49%)
  local copies, waits for them, and re-layouts  50.8 us (20%)
  matrix products  27.5 us (11%)
  waiting for transfers between devices  21.8 us (9%)
  starting transfers between devices  13.8 us (5%)
  other arithmetic  11.4 us (5%)
    psum x2, blocking collectives, on_device(): gram = lax.psum(lax.psum(partial_gram, 'grid'), 'orb')  64.3 us
    unnamed x1, blocking collectives  29.9 us
    all_gather x1, blocking collectives, on_device(): lax.all_gather(whole, 'orb', axis=0, tiled=True)  24.3 us
    transpose x1, local copies, waits for them, and re-layouts, solve_pairs(): jnp.einsum('ax,pxyz->payz', table_x, section, preferred_element_type=jnp....  12.1 us
    dot_general x2, matrix products, solve_pairs(): jnp.einsum('by,pxyz->pxbz', table_y, section, preferred_element_type=jnp....  10.6 us
    convert_element_type x1, local copies, waits for them, and re-layouts, solve_pairs(): section = jnp.einsum('by,pxyz->pxbz', table_y, section, preferred_element...  10.1 us
    convert_element_type x1, local copies, waits for them, and re-layouts, solve_pairs(): section = jnp.einsum('ax,pxyz->payz', table_x, density, preferred_element...  8.51 us
    convert_element_type x2, local copies, waits for them, and re-layouts, accumulate(): source_rows = sources.astype(jnp.float32)  7.76 us
  transfers between devices with their start and end apart: 4, of which 4 were waited for; matrix products, arithmetic and copies ran while one was open for 1% of the time, Pallas kernels for 0%

profile of v1, /device:TPU:0, one launch (start us, length us, event | category | flops | bytes accessed | tf_op | source)
XLA Modules:
  0.0 250.9 jit_solution(6524610204877749692)
XLA Ops:
  0.7 5.7 %all_gather.10 = bf16[2,11520]{1,0:T(2,128)(2,1)S(1)} all-gather(bf16[2,5760]{1,0:T(2,128)(2,1)} %param.2), channel_id=1, replica_groups=mesh['orb'=16,'grid'=2] {'grid'}, dimensions={1}, use_global_device_ids=true | all-gather | bytes 69120 | tf_op jit(solution)/shard_map/all_gather | solution.py:86
  6.3 24.3 %all-gather = bf16[16,2,11520]{2,1,0:T(2,128)(2,1)S(1)} all-gather(bf16[1,2,11520]{2,1,0:T(2,128)(2,1)S(1)} %bitcast.58), channel_id=1, replica_groups=mesh['orb'=16,'grid'=2] {'orb'}, dimensions={0}, use_global_device_ids=true | all-gather | bytes 783360 | tf_op jit(solution)/shard_map/all_gather | solution.py:92
  30.7 6.4 %reshape.167 = f32[32,20,24,24]{3,2,1,0:T(8,128)} reshape(bf16[16,2,11520]{2,1,0:T(2,128)(2,1)S(1)} %all-gather) | data formatting | bytes 2211840 | tf_op jit(solution)/shard_map/while/body/eval_jaxpr/convert_element_type | solution.py:69
  37.1 1.3 reshape.174
  38.4 0.1 convert_reduce_fusion
  38.6 0.2 reshape.166
  38.8 3.9 %multiply_convert_fusion.1 = bf16[32,20,24,24]{3,2,1,0:T(8,128)(2,1)S(1)} fusion(f32[32,20,24,24]{3,2,1,0:T(8,128)} %reshape.167, f32[20,24,24]{2,1,0:T(8,128)S(1)} %reshape.166), kind=kLoop, calls=%fused_computation.1 | loop fusion | flops 737280 | bytes 2257920 | tf_op jit(solution)/shard_map/while/body/eval_jaxpr/convert_element_type | solution.py:70
  42.6 4.9 %convert_bitcast_fusion = bf16[32,20,24,24]{1,3,2,0:T(8,128)(2,1)} fusion(bf16[32,20,24,24]{3,2,1,0:T(8,128)(2,1)S(1)} %multiply_convert_fusion.1), kind=kOutput, calls=%fused_computation.4 | convolution fusion | flops 15118640 | bytes 1474560 | tf_op jit(solution)/shard_map/while/body/eval_jaxpr/ax,pxyz->payz/dot_general | solution.py:37
  47.5 8.5 %copy.24 = bf16[32,20,24,24]{2,3,1,0:T(8,128)(2,1)} copy(bf16[32,20,24,24]{1,3,2,0:T(8,128)(2,1)} %convert_bitcast_fusion) | data formatting | bytes 1474560 | tf_op jit(solution)/shard_map/while/body/eval_jaxpr/convert_element_type | solution.py:39
  56.0 5.2 %fusion.44 = bf16[32,20,24,24]{3,2,1,0:T(8,128)(2,1)} fusion(bf16[32,20,24,24]{2,3,1,0:T(8,128)(2,1)} %copy.24), kind=kOutput, calls=%fused_computation.53 | convolution fusion | flops 17701056 | bytes 1474560 | tf_op jit(solution)/shard_map/while/body/eval_jaxpr/by,pxyz->pxbz/dot_general | solution.py:40
  61.3 0.1 fusion.19
  61.5 7.4 %fusion.2 = bf16[32,20,24,24]{3,2,1,0:T(8,128)(2,1)} fusion(f32[20,24,24]{2,1,0:T(8,128)S(1)} %fusion.19, bf16[32,20,24,24]{3,2,1,0:T(8,128)(2,1)} %fusion.44), kind=kOutput, calls=%fused_computation.5 | convolution fusion | flops 36139392 | bytes 1520640 | tf_op jit(solution)/shard_map/while/body/eval_jaxpr/cz,pxyz->pxyc/dot_general | solution.py:45
  68.9 5.4 %convert_bitcast_fusion.1 = bf16[32,20,24,24]{2,3,1,0:T(8,128)(2,1)} fusion(bf16[32,20,24,24]{3,2,1,0:T(8,128)(2,1)} %fusion.2), kind=kOutput, calls=%fused_computation.8 | convolution fusion | flops 18069696 | bytes 1474560 | tf_op jit(solution)/shard_map/while/body/eval_jaxpr/by,pxyz->pxbz/dot_general | solution.py:48
  74.3 10.1 %copy.27 = bf16[32,20,24,24]{0,1,3,2:T(8,128)(2,1)S(1)} copy(bf16[32,20,24,24]{2,3,1,0:T(8,128)(2,1)} %convert_bitcast_fusion.1) | data formatting | bytes 1474560 | tf_op jit(solution)/shard_map/while/body/eval_jaxpr/convert_element_type | solution.py:50
  84.4 4.0 %convolution_bitcast_fusion = f32[32,20,24,24]{0,1,3,2:T(8,128)} fusion(bf16[32,20,24,24]{0,1,3,2:T(8,128)(2,1)S(1)} %copy.27), kind=kOutput, calls=%fused_computation.13 | convolution fusion | flops 14750000 | bytes 2211840 | tf_op jit(solution)/shard_map/while/body/eval_jaxpr/ax,pxyz->payz/dot_general | solution.py:51
  88.4 12.1 %copy.28 = f32[32,20,24,24]{3,2,1,0:T(8,128)} copy(f32[32,20,24,24]{0,1,3,2:T(8,128)} %convolution_bitcast_fusion) | data formatting | bytes 2949120 | tf_op jit(solution)/shard_map/while/body/eval_jaxpr/ax,pxyz->payz/transpose | solution.py:51
  100.5 0.6 dynamic-slice
  101.8 0.2 dynamic-update-slice.3
  102.0 6.8 %reshape.165 = f32[32,11520]{1,0:T(8,128)S(1)} reshape(f32[32,20,24,24]{3,2,1,0:T(8,128)} %copy.28) | data formatting | bytes 2949120 | tf_op jit(solution)/shard_map/while/body/eval_jaxpr/reshape | solution.py:72
  108.9 29.9 %all-reduce = bf16[32]{0:T(256)(128)(2,1)S(1)} all-reduce(bf16[32]{0:T(256)(128)(2,1)S(1)} %dynamic-update-slice.3), channel_id=1, replica_groups=mesh['orb'=16,'grid'=2] {'orb'}, use_global_device_ids=true, to_apply=%add | all-reduce | flops 32 | bytes 128
  138.8 0.3 multiply_reduce_fusion
  139.1 0.7 sub.25
  139.7 3.3 %all-to-all-start = ((f32[1,2,5760]{2,0,1:T(1,128)}), f32[1,2,5760]{2,0,1:T(1,128)S(1)}, u32[]{:S(2)}, u32[]{:S(2)}) async-start(f32[1,2,5760]{2,0,1:T(1,128)} %sub.25), calls=%async_computation | async-start | bytes 92160 | tf_op jit(solution)/shard_map/all_to_all | solution.py:96
  143.0 0.1 reshape.168
  143.2 0.6 copy.30
  143.8 3.2 %all-to-all-done = f32[1,2,5760]{2,0,1:T(1,128)S(1)} async-done(((f32[1,2,5760]{2,0,1:T(1,128)}), f32[1,2,5760]{2,0,1:T(1,128)S(1)}, u32[]{:S(2)}, u32[]{:S(2)}) %all-to-all-start) | async-done | bytes 46112 | tf_op jit(solution)/shard_map/all_to_all | solution.py:96
  147.0 3.5 %all-to-all-start.2 = ((f32[2,16,360]{2,0,1:T(2,128)}), f32[2,16,360]{2,0,1:T(2,128)S(1)}, u32[]{:S(2)}, u32[]{:S(2)}) async-start(f32[2,16,360]{2,0,1:T(2,128)} %copy.30), calls=%async_computation.2 | async-start | bytes 98304 | tf_op jit(solution)/shard_map/all_to_all | solution.py:98
  150.5 0.1 reduce.11
  150.7 0.1 all_to_all.54
  150.8 0.6 copy.29
  151.4 5.8 %all-to-all-done.2 = f32[2,16,360]{2,0,1:T(2,128)S(1)} async-done(((f32[2,16,360]{2,0,1:T(2,128)}), f32[2,16,360]{2,0,1:T(2,128)S(1)}, u32[]{:S(2)}, u32[]{:S(2)}) %all-to-all-start.2) | async-done | bytes 46112 | tf_op jit(solution)/shard_map/all_to_all | solution.py:98
  157.3 3.5 %all-to-all-start.1 = ((f32[2,16,360]{2,0,1:T(2,128)}), f32[2,16,360]{2,0,1:T(2,128)S(1)}, u32[]{:S(2)}, u32[]{:S(2)}) async-start(f32[2,16,360]{2,0,1:T(2,128)} %copy.29), calls=%async_computation.1 | async-start | bytes 98304 | tf_op jit(solution)/shard_map/all_to_all | solution.py:101
  160.8 6.7 %all-to-all-done.1 = f32[2,16,360]{2,0,1:T(2,128)S(1)} async-done(((f32[2,16,360]{2,0,1:T(2,128)}), f32[2,16,360]{2,0,1:T(2,128)S(1)}, u32[]{:S(2)}, u32[]{:S(2)}) %all-to-all-start.1) | async-done | bytes 46112 | tf_op jit(solution)/shard_map/all_to_all | solution.py:101
  167.6 0.2 fusion.17
  167.8 6.7 %psum.14 = f32[32,32]{0,1:T(8,128)S(1)} all-reduce(f32[32,32]{0,1:T(8,128)S(1)} %fusion.17), channel_id=1, replica_groups=mesh['orb'=16,'grid'=2] {'grid'}, use_global_device_ids=true, to_apply=%region_1.2 | all-reduce | flops 1024 | bytes 8192 | tf_op jit(solution)/shard_map/psum | solution.py:112
  174.5 57.6 %psum.15 = f32[32,32]{0,1:T(8,128)S(1)} all-reduce(f32[32,32]{0,1:T(8,128)S(1)} %psum.14), channel_id=1, replica_groups=mesh['orb'=16,'grid'=2] {'orb'}, use_global_device_ids=true, to_apply=%region_2.3 | all-reduce | flops 1024 | bytes 8192 | tf_op jit(solution)/shard_map/psum | solution.py:112
  232.1 0.1 copy.31
  232.2 2.9 %cholesky.17 = f32[32,32]{1,0:T(8,128)S(1)} custom-call(f32[32,32]{1,0:T(8,128)S(1)} %fusion.22), custom_call_target="Cholesky" | custom-call | tf_op jit(solution)/shard_map/jit(cholesky)/cholesky | solution.py:113
  235.1 0.6 compare_reduce_fusion
  235.8 0.7 fusion.21
  236.4 2.4 custom-call.6
  238.9 0.2 fusion.23
  239.1 0.2 fusion.88
  239.3 0.6 copy.34
  239.9 3.5 %all-to-all-start.3 = ((f32[16,2,360]{2,1,0:T(2,128)}), f32[16,2,360]{2,1,0:T(2,128)S(1)}, u32[]{:S(2)}, u32[]{:S(2)}) async-start(f32[16,2,360]{2,1,0:T(2,128)} %copy.34), calls=%async_computation.3 | async-start | bytes 98304 | tf_op jit(solution)/shard_map/all_to_all | solution.py:117
  243.4 0.6 copy.48
  244.1 6.1 %all-to-all-done.3 = f32[16,2,360]{2,1,0:T(2,128)S(1)} async-done(((f32[16,2,360]{2,1,0:T(2,128)}), f32[16,2,360]{2,1,0:T(2,128)S(1)}, u32[]{:S(2)}, u32[]{:S(2)}) %all-to-all-start.3) | async-done | bytes 46112 | tf_op jit(solution)/shard_map/all_to_all | solution.py:117
  250.2 0.8 all_to_all.65
  (22 shorter events, 0.3 us)
Async XLA Ops:
  88.4 12.1 %copy-start.3 = (u32[32]{0:T(128)S(1)}, u32[32]{0:T(128)}, u32[]{:S(2)}) copy-start(u32[32]{0:T(128)} %constant.125) | copy-start | bytes 388
  88.4 13.4 %copy-start.2 = (bf16[2]{0:T(256)(128)(2,1)S(1)}, bf16[2]{0:T(256)(128)(2,1)}, u32[]{:S(2)}) copy-start(bf16[2]{0:T(256)(128)(2,1)} %param.3) | copy-start | bytes 16
  102.0 36.7 %copy-start = (f32[32,11520]{1,0:T(8,128)S(1)}, f32[32,11520]{1,0:T(8,128)}, u32[]{:S(2)}) copy-start(f32[32,11520]{1,0:T(8,128)} %reshape.174) | copy-start | bytes 4423684
  102.0 41.0 %copy-start.1 = (bf16[2,5760]{1,0:T(2,128)(2,1)S(1)}, bf16[2,5760]{1,0:T(2,128)(2,1)}, u32[]{:S(2)}) copy-start(bf16[2,5760]{1,0:T(2,128)(2,1)} %param.2) | copy-start | bytes 69124
  139.7 7.3 %all-to-all-start = ((f32[1,2,5760]{2,0,1:T(1,128)}), f32[1,2,5760]{2,0,1:T(1,128)S(1)}, u32[]{:S(2)}, u32[]{:S(2)}) async-start(f32[1,2,5760]{2,0,1:T(1,128)} %sub.25), calls=%async_computation | async-start | bytes 92160 | tf_op jit(solution)/shard_map/all_to_all | solution.py:96
  147.0 10.2 %all-to-all-start.2 = ((f32[2,16,360]{2,0,1:T(2,128)}), f32[2,16,360]{2,0,1:T(2,128)S(1)}, u32[]{:S(2)}, u32[]{:S(2)}) async-start(f32[2,16,360]{2,0,1:T(2,128)} %copy.30), calls=%async_computation.2 | async-start | bytes 98304 | tf_op jit(solution)/shard_map/all_to_all | solution.py:98
  157.3 10.2 %all-to-all-start.1 = ((f32[2,16,360]{2,0,1:T(2,128)}), f32[2,16,360]{2,0,1:T(2,128)S(1)}, u32[]{:S(2)}, u32[]{:S(2)}) async-start(f32[2,16,360]{2,0,1:T(2,128)} %copy.29), calls=%async_computation.1 | async-start | bytes 98304 | tf_op jit(solution)/shard_map/all_to_all | solution.py:101
  239.9 10.2 %all-to-all-start.3 = ((f32[16,2,360]{2,1,0:T(2,128)}), f32[16,2,360]{2,1,0:T(2,128)S(1)}, u32[]{:S(2)}, u32[]{:S(2)}) async-start(f32[16,2,360]{2,1,0:T(2,128)} %copy.34), calls=%async_computation.3 | async-start | bytes 98304 | tf_op jit(solution)/shard_map/all_to_all | solution.py:117
